TPU v7x, 32 devices: a whole 2x2x4 slice. The times are simulated.
32 devices in a mesh: leaf: 8 (over z, x), blk: 4 (over y, core).
Axes of the slice: x: 2, y: 2, z: 4, core: 2. Of those that a mesh axis runs over, the one named last changes fastest.
Arguments:
- desc_panel: bfloat16 [256, 384, 128], P(('leaf', 'blk')), may hold values from -18 to 18
- row_map: int32 [256, 3], P(('leaf', 'blk')), may hold values from 0 to 55, as said below
- anc_order: int32 [8], replicated, may hold values from 0 to 7, as said below
- anc_below: int32 [8, 12], replicated, may hold values from 32 to 55, as said below
- anc_panel: float32 [8, 4, 4, 128, 512], P('leaf', None, 'blk'), may hold values from -6 to 27, as said below
Outputs:
- chol_panel: float32 [8, 4, 4, 128, 512], P('leaf', None, 'blk')
Inputs may be any that keep to these rules, and one draw needn't show every extreme that they name: `row_map`: entry 0 of each row is a column block of one ancestor; the other entries are distinct entries of that ancestor's row of anc_below. Over the descendants of one device, entry 0 names the column blocks of any one ancestor at most 2 times, and of some ancestor exactly 2 times. `anc_order`: each leaf index holds a different column range. `anc_below`: each row holds 12 distinct indices. `anc_panel`: the leading 512 rows of each ancestor's panel are symmetric, and the leading block of S stays positive definite.
All inputs are finite; a program needn't handle non-finite values.
Results may differ from a plain program's by a relative error of at most 0.0003.
Values may be sent and summed in bfloat16 or wider, within the bound.
A program may use at most 192 MiB of HBM per device.

v0:
```python
import jax
import jax.numpy as jnp
from jax import lax
from jax.sharding import PartitionSpec as P

SLOTS = 2
slot_group = 16


def leaf_owner(ranges, anc_order):
    leaves = jnp.arange(anc_order.shape[0], dtype=jnp.int32)
    return jnp.sum(jnp.where(anc_order[None, :] == ranges[:, None], leaves[None, :], 0), axis=1)


def block_positions(block_ids, owner_leaf, anc_order, anc_below, column_blocks, position_count):
    column_base = anc_order[owner_leaf] * column_blocks
    relative = block_ids - column_base[:, None]
    in_columns = (relative >= 0) & (relative < column_blocks)
    below_ids = anc_below[owner_leaf]
    matching = block_ids[:, :, None] == below_ids[:, None, :]
    offsets = column_blocks + jnp.arange(below_ids.shape[1], dtype=jnp.int32)
    below_place = jnp.sum(jnp.where(matching, offsets[None, None, :], 0), axis=2)
    located = jnp.any(matching, axis=2)
    return jnp.where(in_columns, relative, jnp.where(located, below_place, position_count))


def place_blocks(running, group_place, group_products):
    return running + jnp.einsum(
        "kq,kxy->qxy", group_place, group_products, precision=lax.Precision.HIGHEST
    )


def shards(desc_panel, row_map, anc_order, anc_below, anc_panel):
    leaf_count = lax.axis_size("leaf")
    blk_count = lax.axis_size("blk")
    desc_count, block_count = row_map.shape
    block_rows = anc_panel.shape[3]
    panel_width = anc_panel.shape[4]
    wide_desc = desc_panel.shape[2]
    column_blocks = panel_width // block_rows
    position_count = column_blocks + anc_below.shape[1]
    slot_count = leaf_count * SLOTS
    group_count = slot_count // slot_group
    owner_leaf = leaf_owner(row_map[:, 0] // column_blocks, anc_order)
    positions = block_positions(
        row_map, owner_leaf, anc_order, anc_below, column_blocks, position_count
    )
    desc_index = jnp.arange(desc_count, dtype=jnp.int32)
    same_owner = owner_leaf[:, None] == owner_leaf[None, :]
    earlier = desc_index[None, :] < desc_index[:, None]
    ranking = jnp.sum(same_owner & earlier, axis=1)
    slot_of = owner_leaf * SLOTS + ranking
    matches = slot_of[None, :] == jnp.arange(slot_count, dtype=jnp.int32)[:, None]
    filled = jnp.any(matches, axis=1)
    chosen = jnp.sum(jnp.where(matches, desc_index[None, :], 0), axis=1)
    picked = jnp.where(filled, chosen, desc_count)
    slot_codes = jnp.where(filled[:, None], positions[chosen], position_count).reshape(
        leaf_count, SLOTS, block_count
    )
    send_rows = jnp.take(desc_panel, picked, axis=0, mode="fill", fill_value=0)
    send_rows = send_rows.reshape(leaf_count, SLOTS, block_count * block_rows, wide_desc)
    received, received_codes = (
        lax.all_to_all(send_rows, "leaf", split_axis=0, concat_axis=0, tiled=True),
        lax.all_to_all(
            slot_codes.astype(jnp.bfloat16), "leaf", split_axis=0, concat_axis=0, tiled=True
        ),
    )
    slot_data = received.reshape(group_count, slot_group, block_count * block_rows, wide_desc)

    def accumulate(running, element):
        group_data, group_place = element
        products = jnp.einsum(
            "kaw,kyw->kay",
            group_data,
            group_data[:, :block_rows],
            preferred_element_type=jnp.float32,
        )
        products = products.reshape(slot_group * block_count, block_rows, block_rows)
        return (place_blocks(running, group_place, products), None)

    codes_int = received_codes.astype(jnp.int32).reshape(slot_count, block_count)
    target = codes_int * column_blocks + codes_int[:, :1]
    placing = (
        target[:, :, None]
        == jnp.arange(position_count * column_blocks, dtype=jnp.int32)[None, None, :]
    ).astype(jnp.float32)
    placing = placing.reshape(group_count, slot_group * block_count, position_count * column_blocks)
    initial = jnp.zeros((position_count * column_blocks, block_rows, block_rows), jnp.float32)
    running, _ = lax.scan(accumulate, initial, (slot_data, placing))
    update = running.reshape(position_count, column_blocks, block_rows, block_rows).transpose(
        0, 2, 1, 3
    )
    update = update.reshape(position_count // blk_count, blk_count, block_rows, panel_width)
    local_rows = anc_panel[0]
    mine = lax.axis_index("blk")
    marker = (jnp.arange(blk_count, dtype=jnp.int32) == mine).astype(jnp.float32)
    combined = update - local_rows * marker[None, :, None, None]
    summed = lax.psum(combined, "blk")
    diagonal = -summed.reshape(position_count * block_rows, panel_width)[:panel_width]
    own_rows = -lax.dynamic_slice_in_dim(summed, mine, 1, 1)
    lower_factor = jnp.linalg.cholesky(diagonal)
    panel_rows = own_rows.reshape(-1, panel_width)
    solved = jax.scipy.linalg.solve_triangular(lower_factor, panel_rows.T, lower=True).T
    return solved.reshape(anc_panel.shape)


def solution(mesh):
    in_specs = (
        P(("leaf", "blk"), None, None),
        P(("leaf", "blk"), None),
        P(),
        P(),
        P("leaf", None, "blk", None, None),
    )
    out_specs = P("leaf", None, "blk", None, None)
    return jax.shard_map(shards, mesh=mesh, in_specs=in_specs, out_specs=out_specs, check_vma=False)
```

profile of v0, /device:TPU:0, one launch (start us, length us, event | category | flops | bytes accessed | tf_op | source)
XLA Modules:
  0.0 327.3 jit_solution(11401863305329569041)
XLA Ops:
  15.5 7.3 %all-to-all-start = ((bf16[8,2,3]{2,1,0:T(2,128)(2,1)}), bf16[8,2,3]{2,1,0:T(2,128)(2,1)S(1)}, u32[]{:S(2)}, u32[]{:S(2)}) async-start(bf16[8,2,3]{2,1,0:T(2,128)(2,1)} %copy.58), calls=%async_computation | async-start | bytes 8192 | tf_op jit(solution)/shard_map/all_to_all | solution.py:64
  25.0 4.1 %all-to-all-done = bf16[8,2,3]{2,1,0:T(2,128)(2,1)S(1)} async-done(((bf16[8,2,3]{2,1,0:T(2,128)(2,1)}), bf16[8,2,3]{2,1,0:T(2,128)(2,1)S(1)}, u32[]{:S(2)}, u32[]{:S(2)}) %all-to-all-start) | async-done | bytes 128 | tf_op jit(solution)/shard_map/all_to_all | solution.py:64
  29.2 3.6 %all-to-all-start.1 = ((bf16[8,2,384,128]{3,2,1,0:T(8,128)(2,1)}), bf16[8,2,384,128]{3,2,1,0:T(8,128)(2,1)S(1)}, u32[]{:S(2)}, u32[]{:S(2)}) async-start(bf16[8,2,384,128]{3,2,1,0:T(8,128)(2,1)} %broadcast_select_fusion), calls=%async_computation.1 | async-start | bytes 3145728 | tf_op jit(solution)/shard_map/all_to_all | solution.py:63
  32.8 1.6 copy.62
  34.8 33.9 %all-to-all-done.1 = bf16[8,2,384,128]{3,2,1,0:T(8,128)(2,1)S(1)} async-done(((bf16[8,2,384,128]{3,2,1,0:T(8,128)(2,1)}), bf16[8,2,384,128]{3,2,1,0:T(8,128)(2,1)S(1)}, u32[]{:S(2)}, u32[]{:S(2)}) %all-to-all-start.1) | async-done | bytes 1572896 | tf_op jit(solution)/shard_map/all_to_all | solution.py:63
  69.3 6.0 %fusion.3 = f32[16,128,4,128]{3,0,1,2:T(8,128)} fusion(f32[48,128,128]{2,1,0:T(8,128)S(1)} %bitcast.107, s32[16,4]{0,1:T(4,128)S(1)} %multiply_add_fusion, s32[48]{0:T(128)S(1)} %add.130), kind=kOutput, calls=%fused_computation.10 | convolution fusion | flops 603982848 | bytes 7340480 | tf_op jit(solution)/shard_map/while/body/eval_jaxpr/kq,kxy->qxy/dot_general | solution.py:28
  75.3 5.7 %copy.61 = f32[16,128,4,128]{1,3,2,0:T(8,128)} copy(f32[16,128,4,128]{3,0,1,2:T(8,128)} %fusion.3) | data formatting | bytes 8388608 | tf_op jit(solution)/shard_map/transpose | solution.py:90
  80.9 4.7 %multiply_subtract_fusion = f32[4,4,128,512]{2,3,1,0:T(8,128)} fusion(f32[4,4,128,512]{2,3,1,0:T(8,128)} %bitcast.106, f32[4]{0:T(128)S(1)} %compare_convert_fusion, f32[4,128,512]{1,2,0:T(8,128)S(1)} %copy.62), kind=kLoop, calls=%fused_computation.6 | loop fusion | flops 2097152 | bytes 9437200 | tf_op jit(solution)/shard_map/sub | solution.py:97
  85.7 84.5 %all-reduce.3.cloned.1.call-done = f32[4,4,128,512]{2,3,1,0:T(8,128)} async-done(((f32[4,4,128,512]{2,3,1,0:T(8,128)}), f32[4,4,128,512]{2,3,1,0:T(8,128)}) %all-reduce.3.cloned.1.call-update) | async-done | bytes 4194320 | tf_op jit(solution)/shard_map/psum | solution.py:98
  173.2 1.6 copy.64
  175.9 11.7 %cholesky.104 = f32[128,128]{1,0:T(8,128)S(1)} custom-call(f32[128,128]{1,0:T(8,128)S(1)} %cholesky.266), custom_call_target="Cholesky" | custom-call | tf_op jit(solution)/shard_map/jit(cholesky)/cholesky | solution.py:101
  187.8 9.8 %custom-call.31 = f32[1,128,128]{1,2,0:T(8,128)S(1)} custom-call(f32[1,128,128]{2,1,0:T(8,128)S(1)} %get-tuple-element.44), custom_call_target="InvertDiagBlocksLowerTriangular" | custom-call | tf_op jit(solution)/shard_map/jit(cholesky)/cholesky | solution.py:101
  200.1 11.9 %cholesky.217 = f32[128,128]{1,0:T(8,128)S(1)} custom-call(f32[128,128]{1,0:T(8,128)S(1)} %cholesky.270), custom_call_target="Cholesky" | custom-call | tf_op jit(solution)/shard_map/jit(cholesky)/cholesky | solution.py:101
  213.4 9.8 %custom-call.32 = f32[1,128,128]{1,2,0:T(8,128)S(1)} custom-call(f32[1,128,128]{2,1,0:T(8,128)S(1)} %get-tuple-element.41), custom_call_target="InvertDiagBlocksLowerTriangular" | custom-call | tf_op jit(solution)/shard_map/jit(cholesky)/cholesky | solution.py:101
  224.7 11.7 %cholesky.238 = f32[128,128]{1,0:T(8,128)S(1)} custom-call(f32[128,128]{1,0:T(8,128)S(1)} %cholesky.275), custom_call_target="Cholesky" | custom-call | tf_op jit(solution)/shard_map/jit(cholesky)/cholesky | solution.py:101
  237.2 9.8 %custom-call.33 = f32[1,128,128]{1,2,0:T(8,128)S(1)} custom-call(f32[1,128,128]{2,1,0:T(8,128)S(1)} %get-tuple-element.38), custom_call_target="InvertDiagBlocksLowerTriangular" | custom-call | tf_op jit(solution)/shard_map/jit(cholesky)/cholesky | solution.py:101
  248.5 11.9 %cholesky.255 = f32[128,128]{1,0:T(8,128)S(1)} custom-call(f32[128,128]{1,0:T(8,128)S(1)} %convolution_subtract_fusion.5), custom_call_target="Cholesky" | custom-call | tf_op jit(solution)/shard_map/jit(cholesky)/cholesky | solution.py:101
  263.8 7.9 %while.1 = (s32[]{:T(128)}, f32[512,512]{1,0:T(8,128)S(1)}, s32[4,2]{0,1:T(2,128)S(1)}, f32[4,128,128]{2,1,0:T(8,128)S(1)}, s32[]{:T(128)}) while((s32[]{:T(128)}, f32[512,512]{1,0:T(8,128)S(1)}, s32[4,2]{0,1:T(2,128)S(1)}, f32[4,128,128]{2,1,0:T(8,128)S(1)}, s32[]{:T(128)}) %tuple.30), condition=%wide.while_cond, body=%wide.while_body.sunk | while | flops 2 | bytes 131181 | solution.py:103
  264.4 1.4 bitcast_dynamic-update-slice_fusion.2
  266.4 1.4 bitcast_dynamic-update-slice_fusion.2
  268.3 1.4 bitcast_dynamic-update-slice_fusion.2
  270.3 1.4 bitcast_dynamic-update-slice_fusion.2
  271.7 39.3 %custom-call.34 = f32[4,128,128]{1,2,0:T(8,128)S(1)} custom-call(f32[4,128,128]{2,1,0:T(8,128)S(1)} %get-tuple-element.24), custom_call_target="InvertDiagBlocksLowerTriangular" | custom-call | tf_op jit(solution)/shard_map/jit(_solve_triangular)/triangular_solve | solution.py:103
  316.8 1.6 convolution_subtract_fusion.2
  (93 shorter events, 34.9 us)
Async XLA Ops:
  6.5 16.3 %copy-start = (bf16[8,384,128]{2,1,0:T(8,128)(2,1)S(1)}, bf16[8,384,128]{2,1,0:T(8,128)(2,1)}, u32[]{:S(2)}) copy-start(bf16[8,384,128]{2,1,0:T(8,128)(2,1)} %param.5) | copy-start | bytes 2359300
  15.5 13.7 %all-to-all-start = ((bf16[8,2,3]{2,1,0:T(2,128)(2,1)}), bf16[8,2,3]{2,1,0:T(2,128)(2,1)S(1)}, u32[]{:S(2)}, u32[]{:S(2)}) async-start(bf16[8,2,3]{2,1,0:T(2,128)(2,1)} %copy.58), calls=%async_computation | async-start | bytes 8192 | tf_op jit(solution)/shard_map/all_to_all | solution.py:64
  29.2 39.5 %all-to-all-start.1 = ((bf16[8,2,384,128]{3,2,1,0:T(8,128)(2,1)}), bf16[8,2,384,128]{3,2,1,0:T(8,128)(2,1)S(1)}, u32[]{:S(2)}, u32[]{:S(2)}) async-start(bf16[8,2,384,128]{3,2,1,0:T(8,128)(2,1)} %broadcast_select_fusion), calls=%async_computation.1 | async-start | bytes 3145728 | tf_op jit(solution)/shard_map/all_to_all | solution.py:63
  32.7 137.4 %all-reduce.3.cloned.1.call-start = ((), (), s32[]{:S(2)}) async-start(), calls=%async_computation.2 | async-start | bytes 8388608 | tf_op jit(solution)/shard_map/psum | solution.py:98
  174.9 1.0 copy-start.2
  271.7 39.3 %copy-start.1 = (f32[512,512]{1,0:T(8,128)}, f32[512,512]{1,0:T(8,128)S(1)}, u32[]{:S(2)}) copy-start(f32[512,512]{1,0:T(8,128)S(1)} %get-tuple-element.101) | copy-start | bytes 3145732
Sparse Core Ops, SparseCore 0:
  85.8 84.3 all-reduce.2
where the time goes:
time: 333 us; the launch traced here: 327 us
  other arithmetic  132 us (40%)
  waiting for transfers between devices  123 us (37%)
  local copies, waits for them, and re-layouts  27.7 us (8%)
  matrix products  17.8 us (5%)
  between operations  16.6 us (5%)
  starting transfers between devices  10.9 us (3%)
    psum x1, waiting for transfers between devices, shards(): summed = lax.psum(combined, 'blk')  84.5 us
    another operation x15, other arithmetic, shards(): lower_factor = jnp.linalg.cholesky(diagonal)  79.4 us
    another operation x3, other arithmetic, shards(): jax.scipy.linalg.solve_triangular(lower_factor, panel_rows.T, lower=True)  39.4 us
    all_to_all x1, waiting for transfers between devices, shards(): lax.all_to_all(send_rows, 'leaf', split_axis=0, concat_axis=0, tiled=True)  33.9 us
    another operation x12, local copies, waits for them, and re-layouts  7.81 us
    all_to_all x1, starting transfers between devices, shards(): lax.all_to_all(slot_codes.astype(jnp.bfloat16), 'leaf', split_axis=0, con...  7.28 us
  transfers between devices with their start and end apart: 3, of which 3 were waited for; matrix products, arithmetic and copies ran while one was open for 1% of the time, Pallas kernels for 0%

commit v1 on v0

--- a/solution.py
+++ b/solution.py
@@ -2,9 +2,23 @@
 import jax.numpy as jnp
 from jax import lax
 from jax.sharding import PartitionSpec as P
+from jax.lax import axis_index, axis_size, ppermute
 
 SLOTS = 2
 slot_group = 16
+
+
+def state_quarters(slab_in, on_dim, block_here):
+    everything, arr_next = (slab_in.shape[:on_dim], slab_in.shape[on_dim + 1 :])
+    return jnp.moveaxis(slab_in.reshape(*everything, block_here, -1, *arr_next), on_dim, 0)
+
+
+def _post_works(local_block, dim_i):
+    local_block = jnp.moveaxis(local_block, 0, dim_i)
+    before = local_block.shape
+    return local_block.reshape(
+        *before[:dim_i], before[dim_i] * before[dim_i + 1], *before[dim_i + 2 :]
+    )
 
 
 def leaf_owner(ranges, anc_order):
@@ -31,6 +45,22 @@
 
 
 def shards(desc_panel, row_map, anc_order, anc_below, anc_panel):
+
+    def attach_halves(local, dev_axis, q_in, matrix):
+        out_arr = axis_size(dev_axis)
+        b_now, after = (out_arr, axis_index(dev_axis))
+        t_next = state_quarters(local, matrix, b_now)
+        passed = t_next
+        for it in range(1, b_now):
+            u_next, h_now = ((after + it) % b_now, (after - it) % b_now)
+            block_next = lax.dynamic_index_in_dim(t_next, u_next, 0)
+            oldest = range(b_now)
+            top = map(lambda u: (u, (u + it) % b_now), oldest)
+            last = list(top)
+            carry_in = ppermute(block_next, axis_name=dev_axis, perm=last)
+            passed = lax.dynamic_update_slice_in_dim(passed, carry_in, h_now, axis=0)
+        return _post_works(passed, q_in)
+
     leaf_count = lax.axis_size("leaf")
     blk_count = lax.axis_size("blk")
     desc_count, block_count = row_map.shape
@@ -60,7 +90,7 @@
     send_rows = jnp.take(desc_panel, picked, axis=0, mode="fill", fill_value=0)
     send_rows = send_rows.reshape(leaf_count, SLOTS, block_count * block_rows, wide_desc)
     received, received_codes = (
-        lax.all_to_all(send_rows, "leaf", split_axis=0, concat_axis=0, tiled=True),
+        attach_halves(send_rows, "leaf", 0, 0),
         lax.all_to_all(
             slot_codes.astype(jnp.bfloat16), "leaf", split_axis=0, concat_axis=0, tiled=True
         ),

time: 333 us -> 336 us (level)
  waiting for transfers between devices: 123 us -> 109 us
  starting transfers between devices: 10.9 us -> 18.6 us
  local copies, waits for them, and re-layouts: 27.7 us -> 34 us
    all_to_all x1 -> x0, waiting for transfers between devices: 33.9 us -> none  [shards(): lax.all_to_all(send_rows, 'leaf', split_axis=0, concat_axis=0, tiled=True)]
    ppermute x0 -> x7, starting transfers between devices: none -> 13.7 us  [attach_halves(): carry_in = ppermute(block_next, axis_name=dev_axis, perm=last)]
    ppermute x0 -> x7, waiting for transfers between devices: none -> 13.3 us  [attach_halves(): carry_in = ppermute(block_next, axis_name=dev_axis, perm=last)]
    psum x1, waiting for transfers between devices: 84.5 us -> 95.9 us  [shards(): summed = lax.psum(combined, 'blk')]
    all_to_all x1, waiting for transfers between devices: 4.13 us -> 0.01 us  [shards(): lax.all_to_all(slot_codes.astype(jnp.bfloat16), 'leaf', split_axis=0, con...]
    all_to_all x1 -> x0, starting transfers between devices: 3.58 us -> none  [shards(): lax.all_to_all(send_rows, 'leaf', split_axis=0, concat_axis=0, tiled=True)]
  transfers between devices with their start and end apart: 3 -> 9, of which waited for: 3 -> 5; matrix products, arithmetic and copies ran while one was open for 1% -> 3% of each run, Pallas kernels for 0% -> 0%
where the time goes in v1:
time: 336 us; the launch traced here: 329 us
  other arithmetic  132 us (39%)
  waiting for transfers between devices  109 us (32%)
  local copies, waits for them, and re-layouts  34 us (10%)
  matrix products  18.7 us (6%)
  starting transfers between devices  18.6 us (6%)
  between operations  17 us (5%)
    psum x1, waiting for transfers between devices, shards(): summed = lax.psum(combined, 'blk')  95.9 us
    another operation x15, other arithmetic, shards(): lower_factor = jnp.linalg.cholesky(diagonal)  79.4 us
    another operation x3, other arithmetic, shards(): jax.scipy.linalg.solve_triangular(lower_factor, panel_rows.T, lower=True)  40.3 us
    ppermute x7, starting transfers between devices, attach_halves(): carry_in = ppermute(block_next, axis_name=dev_axis, perm=last)  13.7 us
    ppermute x7, waiting for transfers between devices, attach_halves(): carry_in = ppermute(block_next, axis_name=dev_axis, perm=last)  13.3 us
    another operation x12, local copies, waits for them, and re-layouts  10.3 us
  transfers between devices with their start and end apart: 9, of which 5 were waited for; matrix products, arithmetic and copies ran while one was open for 3% of the time, Pallas kernels for 0%

profile of v1, /device:TPU:0, one launch (start us, length us, event | category | flops | bytes accessed | tf_op | source)
XLA Modules:
  0.0 329.1 jit_solution(17218874917717642073)
XLA Ops:
  12.9 3.0 collective-permute-start
  19.4 4.9 %all-to-all-start = ((bf16[8,2,3]{2,1,0:T(2,128)(2,1)}), bf16[8,2,3]{2,1,0:T(2,128)(2,1)S(1)}, u32[]{:S(2)}, u32[]{:S(2)}) async-start(bf16[8,2,3]{2,1,0:T(2,128)(2,1)} %copy.58), calls=%async_computation | async-start | bytes 8192 | tf_op jit(solution)/shard_map/all_to_all | solution.py:94
  26.2 2.0 constant_dynamic-slice_fusion.1
  30.0 2.4 collective-permute-start.2
  34.3 2.4 collective-permute-start.4
  40.5 9.7 %collective-permute-done.2 = bf16[1,1,2,384,128]{4,3,2,0,1:T(8,128)(2,1)} collective-permute-done((bf16[1,1,2,384,128]{4,3,2,0,1:T(8,128)(2,1)}, bf16[1,1,2,384,128]{4,3,2,0,1:T(8,128)(2,1)}, u32[]{:S(2)}, u32[]{:S(2)}) %collective-permute-start.2) | collective-permute-done | bytes 196640 | tf_op jit(solution)/shard_map/ppermute | solution.py:60
  51.1 2.1 collective-permute-done.3
  55.3 6.0 %fusion.3 = f32[16,128,4,128]{3,0,1,2:T(8,128)} fusion(f32[48,128,128]{2,1,0:T(8,128)S(1)} %bitcast.108, s32[16,4]{0,1:T(4,128)S(1)} %multiply_add_fusion, s32[48]{0:T(128)S(1)} %add.244), kind=kOutput, calls=%fused_computation.10 | convolution fusion | flops 603982848 | bytes 7340480 | tf_op jit(solution)/shard_map/while/body/eval_jaxpr/kq,kxy->qxy/dot_general | solution.py:42
  61.4 5.7 %copy.61 = f32[16,128,4,128]{1,3,2,0:T(8,128)} copy(f32[16,128,4,128]{3,0,1,2:T(8,128)} %fusion.3) | data formatting | bytes 8388608 | tf_op jit(solution)/shard_map/transpose | solution.py:120
  67.0 4.7 %multiply_subtract_fusion = f32[4,4,128,512]{2,3,1,0:T(8,128)} fusion(f32[4,4,128,512]{2,3,1,0:T(8,128)} %bitcast.106, f32[4]{0:T(128)S(1)} %compare_convert_fusion, f32[4,128,512]{1,2,0:T(8,128)S(1)} %copy.62), kind=kLoop, calls=%fused_computation.6 | loop fusion | flops 2097152 | bytes 9437200 | tf_op jit(solution)/shard_map/sub | solution.py:127
  71.7 95.9 %all-reduce.3.cloned.1.call-done = f32[4,4,128,512]{2,3,1,0:T(8,128)} async-done(((f32[4,4,128,512]{2,3,1,0:T(8,128)}), f32[4,4,128,512]{2,3,1,0:T(8,128)}) %all-reduce.3.cloned.1.call-update) | async-done | bytes 4194320 | tf_op jit(solution)/shard_map/psum | solution.py:128
  173.4 11.7 %cholesky.104 = f32[128,128]{1,0:T(8,128)S(1)} custom-call(f32[128,128]{1,0:T(8,128)S(1)} %cholesky.266), custom_call_target="Cholesky" | custom-call | tf_op jit(solution)/shard_map/jit(cholesky)/cholesky | solution.py:131
  185.3 9.8 %custom-call.31 = f32[1,128,128]{1,2,0:T(8,128)S(1)} custom-call(f32[1,128,128]{2,1,0:T(8,128)S(1)} %get-tuple-element.51), custom_call_target="InvertDiagBlocksLowerTriangular" | custom-call | tf_op jit(solution)/shard_map/jit(cholesky)/cholesky | solution.py:131
  197.7 11.9 %cholesky.217 = f32[128,128]{1,0:T(8,128)S(1)} custom-call(f32[128,128]{1,0:T(8,128)S(1)} %cholesky.270), custom_call_target="Cholesky" | custom-call | tf_op jit(solution)/shard_map/jit(cholesky)/cholesky | solution.py:131
  210.9 9.8 %custom-call.32 = f32[1,128,128]{1,2,0:T(8,128)S(1)} custom-call(f32[1,128,128]{2,1,0:T(8,128)S(1)} %get-tuple-element.48), custom_call_target="InvertDiagBlocksLowerTriangular" | custom-call | tf_op jit(solution)/shard_map/jit(cholesky)/cholesky | solution.py:131
  222.3 11.7 %cholesky.238 = f32[128,128]{1,0:T(8,128)S(1)} custom-call(f32[128,128]{1,0:T(8,128)S(1)} %cholesky.275), custom_call_target="Cholesky" | custom-call | tf_op jit(solution)/shard_map/jit(cholesky)/cholesky | solution.py:131
  234.7 9.8 %custom-call.33 = f32[1,128,128]{1,2,0:T(8,128)S(1)} custom-call(f32[1,128,128]{2,1,0:T(8,128)S(1)} %get-tuple-element.45), custom_call_target="InvertDiagBlocksLowerTriangular" | custom-call | tf_op jit(solution)/shard_map/jit(cholesky)/cholesky | solution.py:131
  246.0 11.9 %cholesky.255 = f32[128,128]{1,0:T(8,128)S(1)} custom-call(f32[128,128]{1,0:T(8,128)S(1)} %convolution_subtract_fusion.5), custom_call_target="Cholesky" | custom-call | tf_op jit(solution)/shard_map/jit(cholesky)/cholesky | solution.py:131
  261.3 10.3 %while.1 = (s32[]{:T(128)}, f32[512,512]{1,0:T(8,128)S(1)}, s32[4,2]{0,1:T(2,128)S(1)}, f32[4,128,128]{2,1,0:T(8,128)}, s32[]{:T(128)}) while((s32[]{:T(128)}, f32[512,512]{1,0:T(8,128)S(1)}, s32[4,2]{0,1:T(2,128)S(1)}, f32[4,128,128]{2,1,0:T(8,128)}, s32[]{:T(128)}) %tuple.36), condition=%wide.while_cond, body=%wide.while_body.sunk | while | flops 2 | bytes 132705 | solution.py:133
  261.9 2.0 bitcast_dynamic-update-slice_fusion.2
  264.5 2.0 bitcast_dynamic-update-slice_fusion.2
  267.0 2.0 bitcast_dynamic-update-slice_fusion.2
  269.6 2.0 bitcast_dynamic-update-slice_fusion.2
  271.6 40.2 %custom-call.34 = f32[4,128,128]{1,2,0:T(8,128)S(1)} custom-call(f32[4,128,128]{2,1,0:T(8,128)} %get-tuple-element.24), custom_call_target="InvertDiagBlocksLowerTriangular" | custom-call | tf_op jit(solution)/shard_map/jit(_solve_triangular)/triangular_solve | solution.py:133
  (123 shorter events, 48.8 us)
Async XLA Ops:
  6.5 2.2 copy-start
  10.6 5.3 %copy-start.7 = (s32[8,3]{0,1:T(4,128)S(1)}, s32[8,3]{0,1:T(4,128)}, u32[]{:S(2)}) copy-start(s32[8,3]{0,1:T(4,128)} %param.6) | copy-start | bytes 292
  10.6 5.5 %copy-start.1 = (s32[8]{0:T(128)S(1)}, s32[8]{0:T(128)}, u32[]{:S(2)}) copy-start(s32[8]{0:T(128)} %param.7) | copy-start | bytes 100
  10.6 6.1 %copy-start.6 = (s32[8,12]{1,0:T(8,128)S(1)}, s32[8,12]{1,0:T(8,128)}, u32[]{:S(2)}) copy-start(s32[8,12]{1,0:T(8,128)} %param.8) | copy-start | bytes 1156
  12.9 13.2 %collective-permute-start = (bf16[1,1,2,384,128]{4,3,2,0,1:T(8,128)(2,1)}, bf16[1,1,2,384,128]{4,3,2,0,1:T(8,128)(2,1)}, u32[]{:S(2)}, u32[]{:S(2)}) collective-permute-start(bf16[1,1,2,384,128]{4,3,2,0,1:T(8,128)(2,1)} %constant_dynamic-slice_fusion.7), channel_id=1, source_target_pairs={{0,4},{4,8},{8,12},{12,16},{16,20},{20,24},{24,28},{28,0},{1,5},{5... | collective-permute-start | bytes 589832 | tf_op jit(solution)/shard_map/ppermute | solution.py:60
  19.4 13.0 %all-to-all-start = ((bf16[8,2,3]{2,1,0:T(2,128)(2,1)}), bf16[8,2,3]{2,1,0:T(2,128)(2,1)S(1)}, u32[]{:S(2)}, u32[]{:S(2)}) async-start(bf16[8,2,3]{2,1,0:T(2,128)(2,1)} %copy.58), calls=%async_computation | async-start | bytes 8192 | tf_op jit(solution)/shard_map/all_to_all | solution.py:94
  24.3 143.4 %all-reduce.3.cloned.1.call-start = ((), (), s32[]{:S(2)}) async-start(), calls=%async_computation.1 | async-start | bytes 8388608 | tf_op jit(solution)/shard_map/psum | solution.py:128
  28.2 10.1 %collective-permute-start.1 = (bf16[1,1,2,384,128]{4,3,2,0,1:T(8,128)(2,1)}, bf16[1,1,2,384,128]{4,3,2,0,1:T(8,128)(2,1)}, u32[]{:S(2)}, u32[]{:S(2)}) collective-permute-start(bf16[1,1,2,384,128]{4,3,2,0,1:T(8,128)(2,1)} %get-tuple-element.40), channel_id=1, source_target_pairs={{0,8},{4,12},{8,16},{12,20},{16,24},{20,28},{24,0},{28,4},{1,9},{5... | collective-permute-start | bytes 589832 | tf_op jit(solution)/shard_map/ppermute | solution.py:60
  30.0 20.2 %collective-permute-start.2 = (bf16[1,1,2,384,128]{4,3,2,0,1:T(8,128)(2,1)}, bf16[1,1,2,384,128]{4,3,2,0,1:T(8,128)(2,1)}, u32[]{:S(2)}, u32[]{:S(2)}) collective-permute-start(bf16[1,1,2,384,128]{4,3,2,0,1:T(8,128)(2,1)} %get-tuple-element.39), channel_id=1, source_target_pairs={{0,12},{4,16},{8,20},{12,24},{16,28},{20,0},{24,4},{28,8},{1,13},{... | collective-permute-start | bytes 589832 | tf_op jit(solution)/shard_map/ppermute | solution.py:60
  32.7 20.5 %collective-permute-start.3 = (bf16[1,1,2,384,128]{4,3,2,0,1:T(8,128)(2,1)}, bf16[1,1,2,384,128]{4,3,2,0,1:T(8,128)(2,1)S(1)}, u32[]{:S(2)}, u32[]{:S(2)}) collective-permute-start(bf16[1,1,2,384,128]{4,3,2,0,1:T(8,128)(2,1)} %get-tuple-element.38), channel_id=1, source_target_pairs={{0,16},{4,20},{8,24},{12,28},{16,0},{20,4},{24,8},{28,12},{1,17},{... | collective-permute-start | bytes 589832 | tf_op jit(solution)/shard_map/ppermute | solution.py:60
  34.3 19.0 %collective-permute-start.4 = (bf16[1,1,2,384,128]{4,3,2,0,1:T(8,128)(2,1)}, bf16[1,1,2,384,128]{4,3,2,0,1:T(8,128)(2,1)S(1)}, u32[]{:S(2)}, u32[]{:S(2)}) collective-permute-start(bf16[1,1,2,384,128]{4,3,2,0,1:T(8,128)(2,1)} %get-tuple-element.37), channel_id=1, source_target_pairs={{0,20},{4,24},{8,28},{12,0},{16,4},{20,8},{24,12},{28,16},{1,21},{... | collective-permute-start | bytes 589832 | tf_op jit(solution)/shard_map/ppermute | solution.py:60
  36.6 16.7 %collective-permute-start.5 = (bf16[1,1,2,384,128]{4,3,2,0,1:T(8,128)(2,1)}, bf16[1,1,2,384,128]{4,3,2,0,1:T(8,128)(2,1)S(1)}, u32[]{:S(2)}, u32[]{:S(2)}) collective-permute-start(bf16[1,1,2,384,128]{4,3,2,0,1:T(8,128)(2,1)} %get-tuple-element.36), channel_id=1, source_target_pairs={{0,24},{4,28},{8,0},{12,4},{16,8},{20,12},{24,16},{28,20},{1,25},{... | collective-permute-start | bytes 589832 | tf_op jit(solution)/shard_map/ppermute | solution.py:60
  38.3 16.4 %collective-permute-start.6 = (bf16[1,1,2,384,128]{4,3,2,0,1:T(8,128)(2,1)}, bf16[1,1,2,384,128]{4,3,2,0,1:T(8,128)(2,1)S(1)}, u32[]{:S(2)}, u32[]{:S(2)}) collective-permute-start(bf16[1,1,2,384,128]{4,3,2,0,1:T(8,128)(2,1)} %get-tuple-element.35), channel_id=1, source_target_pairs={{0,28},{4,0},{8,4},{12,8},{16,12},{20,16},{24,20},{28,24},{1,29},{... | collective-permute-start | bytes 589832 | tf_op jit(solution)/shard_map/ppermute | solution.py:60
  172.5 1.0 copy-start.3
  271.6 40.2 %copy-start.2 = (f32[512,512]{1,0:T(8,128)}, f32[512,512]{1,0:T(8,128)S(1)}, u32[]{:S(2)}) copy-start(f32[512,512]{1,0:T(8,128)S(1)} %get-tuple-element.105) | copy-start | bytes 3145732
  311.8 2.1 copy-start.4
  314.3 3.9 %copy-start.5 = (f32[4,128,128]{1,2,0:T(8,128)S(1)}, f32[4,128,128]{1,2,0:T(8,128)}, u32[]{:S(2)}) copy-start(f32[4,128,128]{1,2,0:T(8,128)} %copy-done.4) | copy-start | bytes 786436
Sparse Core Ops, SparseCore 0:
  71.8 95.7 all-reduce.2
